TPU v7x, 512 devices: a whole 4x8x8 slice. The times are simulated.
512 devices in a mesh: leaf: 128 (over y, z, core), rep: 4 (over x).
Axes of the slice: x: 4, y: 8, z: 8, core: 2. Of those that a mesh axis runs over, the one named last changes fastest.
Arguments:
- coords: float32 [8, 131072], P(None, 'leaf'), may hold values from -8 to 8
- skeleton: float32 [8, 16384], P(None, 'leaf'), may hold values from -8 to 8
- transfer: bfloat16 [256, 64, 64], P('leaf'), may hold values from -0.75 to 0.75
- coupling: bfloat16 [1024, 1024], replicated, may hold values from -3 to 3, as said below
- parent: int32 [256], P('leaf'), may hold values from 0 to 15, never falling along the last dimension, each value on 1 to 24 neighbouring positions
- near_mask: int32 [256, 5], P('leaf'), may hold values from 0 to 1, as said below
- noise: float32 [131072], P('leaf'), may hold values from 0.5 to 2
- rhs: float32 [64, 131072], P('rep', 'leaf'), may hold values from -5 to 5
Outputs:
- solution: float32 [64, 131072], P('rep', 'leaf')
- residual: float32 [64, 131072], P('rep', 'leaf')
Inputs may be any that keep to these rules, and one draw needn't show every extreme that they name: `coupling`: symmetric positive semidefinite. `parent`: never falling along the leaves. Slot 2 is 1; near_mask[l, 2 + o] = near_mask[l + o, 2 - o]; slots pointing before the first or after the last leaf are 0.
All inputs are finite; a program needn't handle non-finite values.
Results may differ from a plain program's by a relative error of at most 0.0003.
Values sent between devices are 32-bit elements; how exact they have to be, the bound alone decides.
No kernel may reach another device: no remote copies, remote signals or barrier semaphores. Data moves between devices by JAX's collectives and lax.ppermute only.
A program may use at most 64 MiB of HBM per device.

v0:
```python
import math

import jax
import jax.numpy as jnp
from jax import lax
from jax.experimental import pallas as pl
from jax.experimental.pallas import tpu as pltpu
from jax.sharding import Mesh
from jax.sharding import PartitionSpec as P


LEAF = 512
DIM = 8
RANK = 64
LEVELS = 16
LEAVES_HERE = 2
SLOTS = 5
SPAN = LEAVES_HERE * LEAF
AXES = ("y", "z", "c")
SCALE = math.sqrt(3.0) / 4.0
LOG2E = 1.4426950408889634
CHUNK = 64
SLOTS_KEPT = 2
F32 = jnp.float32
BF16 = jnp.bfloat16


def split(x, parts):
    out = []
    for _ in range(parts):
        piece = x.astype(BF16).astype(F32)
        out.append(piece)
        x = x - piece
    return out


def pair(x):
    hi, lo = split(x, 2)
    return hi.astype(BF16), lo.astype(BF16)


def pair_dot(x, hi, lo, contract=0):
    dims = (((1,), (contract,)), ((), ()))
    xh, xl = split(x, 2)
    both = jnp.concatenate([xh, xl], axis=0).astype(BF16)
    wide = lax.dot_general(both, hi, dims, preferred_element_type=F32)
    low = lax.dot_general(xh.astype(BF16), lo, dims, preferred_element_type=F32)
    return wide[:16] + wide[16:] + low


def features(c):
    n = c.shape[1]
    c = c * SCALE
    p1, p2, p3 = split(c, 3)
    n1, n2, n3 = split(jnp.sum(c * c, axis=0, keepdims=True), 3)
    row = lax.broadcasted_iota(jnp.int32, (8, n), 0)
    def pick(*rows):
        out = jnp.zeros((8, n), F32)
        for at, value in rows:
            out = jnp.where(row == at, value, out)
        return out
    left_norm = pick((0, n1), (1, n2), (2, n3), (3, 1.0), (4, 1.0), (5, 1.0))
    right_norm = pick((0, 1.0), (1, 1.0), (2, 1.0), (3, n1), (4, n2), (5, n3))
    none = jnp.zeros((8, n), F32)
    q1, q2, q3 = -2.0 * p1, -2.0 * p2, -2.0 * p3
    left = jnp.concatenate([p1, p1, p2, p2, p1, p3, left_norm, none], axis=0)
    right = jnp.concatenate([q1, q2, q1, q2, q3, q1, right_norm, none], axis=0)
    return left, right


def matern(left, right):
    d2 = jnp.dot(left, right, preferred_element_type=F32)
    d2 = jnp.maximum(d2, 1e-30)
    s = d2 * lax.rsqrt(d2)
    return (1.0 + s) * jnp.exp2(s * -LOG2E)


VMEM = pl.BlockSpec(memory_space=pltpu.VMEM)
SMEM = pl.BlockSpec(memory_space=pltpu.SMEM)
HBM = pl.BlockSpec(memory_space=pltpu.HBM)
LIMIT = 24 * 1024 * 1024
PAIRS = 4
ROWS_OUT = 24
ROWS_ACROSS = 16 * PAIRS + 8
TAIL = 80
BESIDE = 128 + TAIL


def off_chip(*arrays):
    return [pltpu.with_memory_space_constraint(x, pltpu.HBM) for x in arrays]


def shaped(*dims, dtype=F32):
    return jax.ShapeDtypeStruct(dims, dtype)


def call(kernel, in_specs, outs, scratch=()):
    return pl.pallas_call(
        kernel,
        out_shape=tuple(outs),
        in_specs=in_specs,
        out_specs=tuple(VMEM for _ in outs),
        scratch_shapes=list(scratch),
        compiler_params=pltpu.CompilerParams(vmem_limit_bytes=LIMIT),
    )


def leaf(i):
    return slice(LEAF * i, LEAF * (i + 1))


def halves(x):
    hi, lo = split(x * (1.0 / LEAF), 2)
    return jnp.concatenate([hi, lo], axis=0).astype(BF16)


def own_block(b):
    i = b // 2
    return i, 2 + b % 2


def halo_at(j):
    return j - 2 * ((j >= 4) * 1)


def halo_block(b):
    i = b // 3
    m = i + b % 3
    far = (m >= 2) * 1
    return i, m + 2 * far


def near_field(count, place, mask_ref, left_of, right_of, v_scr, acc_scr, k_scr):
    for b in range(count):
        i, j = place(b)
        slot = b % SLOTS_KEPT
        right = right_of(i)
        for h in range(LEAF // CHUNK):
            rows = slice(CHUNK * h, CHUNK * (h + 1))
            k = matern(left_of(j, rows), right)
            kh = k.astype(BF16)
            k_scr[slot, 0, rows, :] = kh
            k_scr[slot, 1, rows, :] = (k - kh.astype(F32)).astype(BF16)
        v = v_scr[j]
        total = jnp.dot(v, k_scr[slot, 0], preferred_element_type=F32)
        low = jnp.dot(v[:16], k_scr[slot, 1], preferred_element_type=F32)
        acc_scr[i] = acc_scr[i] + mask_ref[i, j - i].astype(F32) * (total[:16] + total[16:] + low)


def fetch(pairs, sems):
    copies = [pltpu.make_async_copy(src, dst, sems.at[n]) for n, (src, dst) in enumerate(pairs)]
    for copy in copies:
        copy.start()
    return copies


def lifted(v, phi_ref):
    return jnp.concatenate(
        [pair_dot(v[:, leaf(i)], phi_ref[i, 0], phi_ref[i, 1], contract=1) for i in range(LEAVES_HERE)], axis=1
    )


def post(parent_ref, up, v, local, send_ref):
    lane = lax.broadcasted_iota(jnp.int32, (8, 128), 1)
    norm = jnp.sum(v * v, axis=1, keepdims=True)
    inner = jnp.sum(v * local, axis=1, keepdims=True)
    tile = jnp.zeros((8, 128), F32)
    for at, value in enumerate(
        (norm[:8], inner[:8], norm[8:], inner[8:], parent_ref[0].astype(F32), parent_ref[1].astype(F32))
    ):
        tile = jnp.where(lane == at, value, tile)
    for d in range(send_ref.shape[0]):
        send_ref[d, :16, :] = up
        send_ref[d, 16:, :] = tile


def paired(tiles):
    lane = lax.broadcasted_iota(jnp.int32, (16, 128), 1)
    whole = [t + pltpu.roll(t, 64, axis=1) for t in tiles]
    return [jnp.where(lane < 64, whole[m], whole[m + 1]) for m in range(0, len(tiles), 2)]


def across_kernel(got_ref, send_ref):
    lane = lax.broadcasted_iota(jnp.int32, (1, 128), 1)
    first = got_ref[0, 16:17, 4:5]
    tiles = [jnp.zeros((16, 128), F32) for _ in range(2 * PAIRS)]
    scalars = jnp.zeros((8, 128), F32)
    for d in range(got_ref.shape[0]):
        slot = jnp.where(lane < 64, got_ref[d, 16:17, 4:5], got_ref[d, 16:17, 5:6]) - first
        piece = got_ref[d, :16, :]
        for s in range(2 * PAIRS):
            tiles[s] = tiles[s] + jnp.where(slot == float(s), piece, 0.0)
        scalars = scalars + got_ref[d, 16:, :]
    scalars = jnp.where(lane == 4, first, scalars)
    tiles = paired(tiles)
    for y in range(send_ref.shape[0]):
        for k in range(PAIRS):
            send_ref[y, 16 * k : 16 * (k + 1), :] = tiles[k]
        send_ref[y, 16 * PAIRS :, :] = scalars


def whole_sums(got_ref):
    lane = lax.broadcasted_iota(jnp.int32, (1, 128), 1)
    half = (lane >= 64).astype(F32)
    tiles = [jnp.zeros((16, 128), F32) for _ in range(LEVELS)]
    scalars = jnp.zeros((8, 128), F32)
    for y in range(got_ref.shape[0]):
        first = got_ref[y, 16 * PAIRS : 16 * PAIRS + 1, 4:5] + half
        for k in range(PAIRS):
            piece = got_ref[y, 16 * k : 16 * (k + 1), :]
            cluster = first + float(2 * k)
            for q in range(LEVELS):
                tiles[q] = tiles[q] + jnp.where(cluster == float(q), piece, 0.0)
        scalars = scalars + got_ref[y, 16 * PAIRS :, :]
    norm = jnp.concatenate([scalars[:, 0:1], scalars[:, 2:3]], axis=0)
    inner = jnp.concatenate([scalars[:, 1:2], scalars[:, 3:4]], axis=0)
    return jnp.concatenate(paired(tiles), axis=1), norm, inner


def coupled_image(got_ref, coupling_ref, img_scr, ready=lambda: None):
    sums, norm, inner = whole_sums(got_ref)
    parts = jnp.concatenate(split(sums, 3), axis=0).astype(BF16)
    ready()
    image = jnp.dot(parts, coupling_ref[...], preferred_element_type=F32)
    image = image[:16] + image[16:32] + image[32:]
    inner = inner + jnp.sum(sums * image, axis=1, keepdims=True)
    for p in range(LEVELS):
        img_scr[p] = image[:, RANK * p : RANK * (p + 1)]
    return norm, inner


def own_far(parent_ref, phi_ref, img_scr):
    return jnp.concatenate(
        [pair_dot(img_scr[parent_ref[i]], phi_ref[i, 0], phi_ref[i, 1]) for i in range(LEAVES_HERE)], axis=1
    )


def pack_kernel(coords_hbm, skeleton_hbm, transfer_hbm, noise_hbm, rhs_hbm, packed_ref, skeleton_ref, transfer_ref,
                noise_ref, sems):
    for copy in fetch(
        (
            (rhs_hbm, packed_ref.at[pl.ds(DIM, 16), :]), (coords_hbm, packed_ref.at[pl.ds(0, DIM), :]),
            (transfer_hbm, transfer_ref), (skeleton_hbm, skeleton_ref), (noise_hbm, noise_ref),
        ),
        sems,
    ):
        copy.wait()


def pack(coords, skeleton, transfer, noise, rhs):
    return call(
        pack_kernel, [HBM] * 5,
        (shaped(24, SPAN), shaped(DIM, 128), shaped(2, RANK, RANK, dtype=BF16), shaped(1, SPAN)),
        (pltpu.SemaphoreType.DMA((5,)),),
    )(*off_chip(coords, skeleton, transfer, noise, rhs))


FLAGS = [pltpu.SMEM((2,), jnp.int32), pltpu.SMEM((2, SLOTS), jnp.int32)]


def prepare_kernel(parent_hbm, mask_hbm, packed_ref, skeleton_ref, transfer_ref, noise_ref,
                   left_ref, right_ref, phi_ref, part_ref, up_ref, diag_ref, tail_ref,
                   parent_ref, mask_ref, v_scr, acc_scr, k_scr, sems):
    flags = fetch(((parent_hbm, parent_ref), (mask_hbm, mask_ref)), sems)
    left, right = features(packed_ref[:DIM, :])
    v = packed_ref[DIM:, :]
    for i in range(LEAVES_HERE):
        left_ref[i] = left[:, leaf(i)].T.astype(BF16)
        right_ref[i] = right[:, leaf(i)].astype(BF16)
        v_scr[2 + i] = halves(v[:, leaf(i)])
    skeleton = skeleton_ref[...]
    sk_left, _ = features(skeleton)
    for i in range(LEAVES_HERE):
        rows = sk_left[:, RANK * i : RANK * (i + 1)].T.astype(BF16)
        bt = matern(rows, right_ref[i]) * (1.0 / math.sqrt(LEAF))
        moved = transfer_ref[i]
        phi = jnp.zeros((RANK, LEAF), F32)
        for part in split(bt, 3):
            phi = phi + lax.dot_general(
                moved, part.astype(BF16), (((0,), (0,)), ((), ())), preferred_element_type=F32
            )
        phi_ref[i, 0], phi_ref[i, 1] = pair(phi)
    tail_ref[:64, :] = jnp.concatenate([transfer_ref[i].astype(F32) for i in range(LEAVES_HERE)], axis=1)
    tail_ref[64:72, :] = skeleton
    up_ref[...] = lifted(v, phi_ref)
    acc_scr[...] = jnp.zeros(acc_scr.shape, F32)
    for flag in flags:
        flag.wait()
    lane = lax.broadcasted_iota(jnp.int32, (8, 128), 1)
    tail_ref[72:, :] = jnp.where(lane < 64, parent_ref[0].astype(F32), parent_ref[1].astype(F32))
    near_field(4, own_block, mask_ref, lambda j, rows: left_ref[j - 2, rows, :], lambda i: right_ref[i], v_scr, acc_scr, k_scr)
    for i in range(LEAVES_HERE):
        count = mask_ref[i, 0]
        for t in range(1, SLOTS):
            count = count + mask_ref[i, t]
        diag_ref[:, leaf(i)] = noise_ref[:, leaf(i)] + count.astype(F32)
        part_ref[:, leaf(i)] = diag_ref[:, leaf(i)] * v[:, leaf(i)] + acc_scr[i]


def prepare(parent, mask, packed, skeleton, transfer, noise):
    return call(
        prepare_kernel, [HBM] * 2 + [VMEM] * 4,
        (
            shaped(2, LEAF, 64, dtype=BF16), shaped(2, 64, LEAF, dtype=BF16), shaped(2, 2, RANK, LEAF, dtype=BF16),
            shaped(16, SPAN), shaped(16, 128), shaped(1, SPAN), shaped(TAIL, 128),
        ),
        FLAGS + [
            pltpu.VMEM((4, 32, LEAF), BF16), pltpu.VMEM((2, 16, LEAF), F32), pltpu.VMEM((SLOTS_KEPT, 2, LEAF, LEAF), BF16), pltpu.SemaphoreType.DMA((2,)),
        ],
    )(*off_chip(parent, mask), packed, skeleton, transfer, noise)


def first_kernel(parent_hbm, mask_hbm, before_ref, after_ref, right_ref, part_ref, up_ref, packed_ref, tail_ref,
                 left_out, right_out, local_ref, beside_ref, send_ref, parent_ref, mask_ref, v_scr, acc_scr, k_scr, sems):
    flags = fetch(((parent_hbm, parent_ref), (mask_hbm, mask_ref)), sems)
    for g, ref in enumerate((before_ref, after_ref)):
        left, right = features(ref[:DIM, :])
        for i in range(LEAVES_HERE):
            left_out[2 * g + i] = left[:, leaf(i)].T.astype(BF16)
            right_out[2 * g + i] = right[:, leaf(i)].astype(BF16)
            v_scr[4 * g + i] = halves(ref[DIM:, leaf(i)])
    for i in range(LEAVES_HERE):
        acc_scr[i] = part_ref[:, leaf(i)]
    beside_ref[128:, :] = tail_ref[...]
    for flag in flags:
        flag.wait()
    near_field(6, halo_block, mask_ref, lambda j, rows: left_out[halo_at(j), rows, :], lambda i: right_ref[i],
               v_scr, acc_scr, k_scr)
    local = jnp.concatenate([acc_scr[i] for i in range(LEAVES_HERE)], axis=1)
    local_ref[...] = local
    for n in range(SPAN // 128):
        beside_ref[16 * n : 16 * (n + 1), :] = local[:, 128 * n : 128 * (n + 1)]
    post(parent_ref, up_ref[...], packed_ref[DIM:, :], local, send_ref)


def first(parent, mask, before, after, right, part, up, packed, tail, peers):
    return call(
        first_kernel, [HBM] * 2 + [VMEM] * 7,
        (
            shaped(4, LEAF, 64, dtype=BF16), shaped(4, 64, LEAF, dtype=BF16),
            shaped(16, SPAN), shaped(BESIDE, 128), shaped(peers, ROWS_OUT, 128),
        ),
        FLAGS + [
            pltpu.VMEM((6, 32, LEAF), BF16), pltpu.VMEM((2, 16, LEAF), F32), pltpu.VMEM((SLOTS_KEPT, 2, LEAF, LEAF), BF16), pltpu.SemaphoreType.DMA((2,)),
        ],
    )(*off_chip(parent, mask), before, after, right, part, up, packed, tail)


def across(got, rows):
    return call(across_kernel, [VMEM], (shaped(rows, ROWS_ACROSS, 128),))(got)[0]


def second_kernel(parent_hbm, mask_hbm, coupling_hbm, got_ref, phi_ref, local_ref, packed_ref, diag_ref,
                  before_ref, after_ref, halo_before_ref, halo_after_ref, left_ref, right_ref,
                  halo_left_ref, halo_right_ref,
                  residual_ref, along_ref, kept_ref, out_ref, send_ref,
                  parent_ref, mask_ref, coupling_scr, img_scr, v_scr, acc_scr, k_scr, bt_scr, sems):
    copies = fetch(((coupling_hbm, coupling_scr), (parent_hbm, parent_ref), (mask_hbm, mask_ref)), sems)
    sides = ((halo_before_ref, before_ref), (halo_after_ref, after_ref))
    for g, (msg_ref, _) in enumerate(sides):
        sk_left, _ = features(msg_ref[192:200, :])
        for i in range(LEAVES_HERE):
            rows = sk_left[:, RANK * i : RANK * (i + 1)].T.astype(BF16)
            bt = matern(rows, halo_right_ref[2 * g + i]) * (1.0 / math.sqrt(LEAF))
            bt_scr[2 * g + i, 0], bt_scr[2 * g + i, 1] = pair(bt)
    norm, inner = coupled_image(got_ref, coupling_scr, img_scr, copies[0].wait)
    step = norm / inner
    copies[1].wait()
    copies[2].wait()
    rhs = packed_ref[DIM:, :]
    along = local_ref[...] + own_far(parent_ref, phi_ref, img_scr)
    residual = rhs - step * along
    along_ref[...] = along
    residual_ref[...] = residual
    lane = lax.broadcasted_iota(jnp.int32, (16, 128), 1)
    kept_ref[...] = jnp.where(lane == 0, norm, jnp.where(lane == 1, step, 0.0))
    for i in range(LEAVES_HERE):
        v_scr[2 + i] = halves(residual[:, leaf(i)])
    for g, (msg_ref, ref) in enumerate(sides):
        for i in range(LEAVES_HERE):
            parent = jnp.max(msg_ref[200:208, RANK * i : RANK * (i + 1)]).astype(jnp.int32)
            moved = msg_ref[128:192, RANK * i : RANK * (i + 1)].astype(BF16)
            pushed = jnp.zeros((16, RANK), F32)
            parts = lax.dot_general(
                jnp.concatenate(split(img_scr[parent], 3), axis=0).astype(BF16), moved, (((1,), (1,)), ((), ())),
                preferred_element_type=F32,
            )
            pushed = parts[:16] + parts[16:32] + parts[32:]
            far = pair_dot(pushed, bt_scr[2 * g + i, 0], bt_scr[2 * g + i, 1])
            local = jnp.concatenate([msg_ref[16 * n : 16 * (n + 1), :] for n in range(4 * i, 4 * (i + 1))], axis=1)
            v_scr[4 * g + i] = halves(ref[DIM:, leaf(i)] - step * (local + far))
    up = lifted(residual, phi_ref)
    acc_scr[...] = jnp.zeros(acc_scr.shape, F32)
    near_field(4, own_block, mask_ref, lambda j, rows: left_ref[j - 2, rows, :], lambda i: right_ref[i], v_scr, acc_scr, k_scr)
    near_field(6, halo_block, mask_ref, lambda j, rows: halo_left_ref[halo_at(j), rows, :], lambda i: right_ref[i],
               v_scr, acc_scr, k_scr)
    near = jnp.concatenate([acc_scr[i] for i in range(LEAVES_HERE)], axis=1)
    local = diag_ref[...] * residual + near
    out_ref[...] = local
    post(parent_ref, up, residual, local, send_ref)


def second(parent, mask, coupling, *arrays, peers):
    return call(
        second_kernel, [HBM] * 3 + [VMEM] * len(arrays),
        (
            shaped(16, SPAN), shaped(16, SPAN), shaped(16, 128), shaped(16, SPAN), shaped(peers, ROWS_OUT, 128),
        ),
        FLAGS + [
            pltpu.VMEM((LEVELS * RANK, LEVELS * RANK), BF16),
            pltpu.VMEM((LEVELS, 16, RANK), F32), pltpu.VMEM((6, 32, LEAF), BF16), pltpu.VMEM((2, 16, LEAF), F32), pltpu.VMEM((SLOTS_KEPT, 2, LEAF, LEAF), BF16),
            pltpu.VMEM((4, 2, RANK, LEAF), BF16), pltpu.SemaphoreType.DMA((3,)),
        ],
    )(*off_chip(parent, mask, coupling), *arrays)


def last_kernel(parent_hbm, coupling_ref, got_ref, phi_ref, local_ref, packed_ref, residual_ref, along_ref, kept_ref,
                solution_ref, out_ref, parent_ref, img_scr, sems):
    flags = fetch(((parent_hbm, parent_ref),), sems)
    norm, inner = coupled_image(got_ref, coupling_ref, img_scr)
    before = kept_ref[:, 0:1]
    first_step = kept_ref[:, 1:2]
    growth = norm / before
    step = norm / (inner - growth * norm / first_step)
    rhs = packed_ref[DIM:, :]
    residual = residual_ref[...]
    solution_ref[...] = first_step * rhs + step * (residual + growth * rhs)
    flags[0].wait()
    applied = local_ref[...] + own_far(parent_ref, phi_ref, img_scr)
    out_ref[...] = residual - step * (applied + growth * along_ref[...])


def last(parent, *arrays):
    return call(
        last_kernel, [HBM] + [VMEM] * len(arrays), (shaped(16, SPAN), shaped(16, SPAN)),
        (FLAGS[0], pltpu.VMEM((LEVELS, 16, RANK), F32), pltpu.SemaphoreType.DMA((1,))),
    )(*off_chip(parent), *arrays)


def beside(x):
    count = lax.axis_size(AXES)
    before = lax.ppermute(x, AXES, [(i, i + 1) for i in range(count - 1)])
    after = lax.ppermute(x, AXES, [(i + 1, i) for i in range(count - 1)])
    return before, after


def exchange(send, *ready):
    row = lax.all_to_all(send, ("z", "c"), 0, 0, tiled=True)
    column, *ready = lax.optimization_barrier((across(row, lax.axis_size("y")), *ready))
    return lax.all_to_all(column, "y", 0, 0, tiled=True), *ready


def per_device(coords, skeleton, transfer, coupling, parent, near_mask, noise, rhs):
    peers = lax.axis_size(("z", "c"))
    packed, skeleton, transfer, noise = pack(coords, skeleton, transfer, noise.reshape(1, SPAN), rhs)
    before, after = beside(packed)
    left, right, phi, part, up, diag, tail = prepare(parent, near_mask, packed, skeleton, transfer, noise)
    halo_left, halo_right, local, message, send = first(
        parent, near_mask, before, after, right, part, up, packed, tail, peers
    )
    halo_before, halo_after = beside(message)
    got, halo_before, halo_after = exchange(send, halo_before, halo_after)
    residual, along, kept, local, send = second(
        parent, near_mask, coupling, got, phi, local, packed, diag, before, after,
        halo_before, halo_after, left, right, halo_left, halo_right, peers=peers,
    )
    (got,) = exchange(send)
    return last(parent, coupling, got, phi, local, packed, residual, along, kept)


def solution(mesh):
    finer = Mesh(mesh.devices.reshape(8, 8, 2, mesh.shape["rep"]), (*AXES, "rep"))
    placed = (
        P(None, AXES),
        P(None, AXES),
        P(AXES, None, None),
        P(),
        P(AXES),
        P(AXES, None),
        P(AXES),
        P("rep", AXES),
    )
    return jax.shard_map(
        per_device,
        mesh=finer,
        in_specs=placed,
        out_specs=(P("rep", AXES), P("rep", AXES)),
        check_vma=False,
    )
```

profile of v0, /device:TPU:1, one launch (start us, length us, event | category | flops | bytes accessed | tf_op | source)
XLA Modules:
  0.0 103.2 jit_solution(9547545691162879888)
XLA Ops:
  0.6 0.9 shard_map.95
  1.5 8.7 %collective-permute-start.1 = (f32[24,1024]{1,0:T(8,128)S(1)}, f32[24,1024]{1,0:T(8,128)S(1)}, u32[]{:S(2)}, u32[]{:S(2)}) collective-permute-start(f32[24,1024]{1,0:T(8,128)S(1)} %get-tuple-element.26.packed_ref), channel_id=1, source_target_pairs={{4,0},{8,4},{12,8},{16,12},{20,16},{24,20},{28,24},{32,28},{36,32}... | collective-permute-start | bytes 294920 | tf_op jit(solution)/shard_map/ppermute | solution.py:443
  10.3 1.9 %collective-permute-start = (f32[24,1024]{1,0:T(8,128)S(1)}, f32[24,1024]{1,0:T(8,128)S(1)}, u32[]{:S(2)}, u32[]{:S(2)}) collective-permute-start(f32[24,1024]{1,0:T(8,128)S(1)} %get-tuple-element.26.packed_ref), channel_id=1, source_target_pairs={{0,4},{4,8},{8,12},{12,16},{16,20},{20,24},{24,28},{28,32},{32,36}... | collective-permute-start | bytes 294920 | tf_op jit(solution)/shard_map/ppermute | solution.py:442
  12.2 3.9 %shard_map.96 = (bf16[2,512,64]{2,1,0:T(8,128)(2,1)S(1)}, bf16[2,64,512]{2,1,0:T(8,128)(2,1)S(1)}, bf16[2,2,64,512]{3,2,1,0:T(8,128)(2,1)S(1)}, f32[16,1024]{1,0...) custom-call(s32[2]{0:T(128)} %parent_hbm.7, s32[2,5]{1,0:T(2,128)} %mask_hbm.5, ...), custom_call_target="tpu_custom_call" | custom-call | tf_op jit(solution)/shard_map/pallas_call | solution.py:301
  16.1 0.0 collective-permute-done.1.after_ref
  16.1 0.0 collective-permute-done.before_ref
  16.1 4.9 %shard_map.97 = (bf16[4,512,64]{2,1,0:T(8,128)(2,1)S(1)}, bf16[4,64,512]{2,1,0:T(8,128)(2,1)S(1)}, f32[16,1024]{1,0:T(8,128)S(1)}, f32[208,128]{1,0:T(8,128)S(1)}, f32[16,24,128]{2,1,0:T(8,128)}) custom-call(s32[2]{0:T(128)} %parent_hbm.7, s32[2,5]{1,0:T(2,128)} %mask_hbm.5, f32[24,1024]{1,0:T(8,128)S(1)} %collective-permute-done.before_ref, ...), custom_call_target="tpu_custom_call" | custom-call | tf_op jit(solution)/shard_map/pallas_call | solution.py:337
  21.0 8.3 %all-to-all-start = ((f32[16,24,128]{2,1,0:T(8,128)}), f32[16,24,128]{2,1,0:T(8,128)S(1)}, u32[]{:S(2)}, u32[]{:S(2)}) async-start(f32[16,24,128]{2,1,0:T(8,128)} %get-tuple-element.34), calls=%async_computation | async-start | bytes 393216 | tf_op jit(solution)/shard_map/all_to_all | solution.py:448
  29.3 2.0 %collective-permute-start.3 = (f32[208,128]{1,0:T(8,128)S(1)}, f32[208,128]{1,0:T(8,128)S(1)}, u32[]{:S(2)}, u32[]{:S(2)}) collective-permute-start(f32[208,128]{1,0:T(8,128)S(1)} %get-tuple-element.35), channel_id=1, source_target_pairs={{4,0},{8,4},{12,8},{16,12},{20,16},{24,20},{28,24},{32,28},{36,32}... | collective-permute-start | bytes 319496 | tf_op jit(solution)/shard_map/ppermute | solution.py:443
  31.3 3.5 %collective-permute-start.2 = (f32[208,128]{1,0:T(8,128)S(1)}, f32[208,128]{1,0:T(8,128)S(1)}, u32[]{:S(2)}, u32[]{:S(2)}) collective-permute-start(f32[208,128]{1,0:T(8,128)S(1)} %get-tuple-element.35), channel_id=1, source_target_pairs={{0,4},{4,8},{8,12},{12,16},{16,20},{20,24},{24,28},{28,32},{32,36}... | collective-permute-start | bytes 319496 | tf_op jit(solution)/shard_map/ppermute | solution.py:442
  34.8 4.6 %all-to-all-done.got_ref = f32[16,24,128]{2,1,0:T(8,128)S(1)} async-done(((f32[16,24,128]{2,1,0:T(8,128)}), f32[16,24,128]{2,1,0:T(8,128)S(1)}, u32[]{:S(2)}, u32[]{:S(2)}) %all-to-all-start) | async-done | bytes 196640 | tf_op jit(solution)/shard_map/all_to_all | solution.py:448
  39.5 0.3 shard_map.98
  39.8 0.0 collective-permute-done.3.halo_after_ref
  39.8 0.0 collective-permute-done.2.halo_before_ref
  39.8 17.9 %all_to_all.20.got_ref = f32[8,72,128]{2,1,0:T(8,128)S(1)} all-to-all(f32[8,72,128]{2,1,0:T(8,128)S(1)} %shard_map.98), channel_id=1, replica_groups=mesh['y'=8,'z'=8,'c'=2,'rep'=4] {'y'}, dimensions={0} | all-to-all | bytes 589824 | tf_op jit(solution)/shard_map/all_to_all | solution.py:450
  57.7 0.0 copy-start
  57.7 9.3 %shard_map.99 = (f32[16,1024]{1,0:T(8,128)S(1)}, f32[16,1024]{1,0:T(8,128)S(1)}, f32[16,128]{1,0:T(8,128)S(1)}, f32[16,1024]{1,0:T(8,128)S(1)}, f32[16,24,128]{2,1,0:T(8,128)S(1)}) custom-call(s32[2]{0:T(128)} %parent_hbm.7, s32[2,5]{1,0:T(2,128)} %mask_hbm.5, bf16[1024,1024]{1,0:T(8,128)(2,1)} %coupling_ref.1, f32[8,72,128]{2,1,0:T(8,128)S(1)} %all_to_all.20.got_ref, ...), custom_call_target="tpu_custom_call" | custom-call | tf_op jit(solution)/shard_map/pallas_call | solution.py:404
  66.9 17.5 %all_to_all.21.got_ref = f32[16,24,128]{2,1,0:T(8,128)S(1)} all-to-all(f32[16,24,128]{2,1,0:T(8,128)S(1)} %get-tuple-element.45), channel_id=1, replica_groups=mesh['y'=8,'z'=8,'c'=2,'rep'=4] {'z','c'}, dimensions={0} | all-to-all | bytes 393216 | tf_op jit(solution)/shard_map/all_to_all | solution.py:448
  84.4 0.3 shard_map.100
  84.7 15.5 %all_to_all.22.got_ref = f32[8,72,128]{2,1,0:T(8,128)S(1)} all-to-all(f32[8,72,128]{2,1,0:T(8,128)S(1)} %shard_map.100), channel_id=1, replica_groups=mesh['y'=8,'z'=8,'c'=2,'rep'=4] {'y'}, dimensions={0} | all-to-all | bytes 589824 | tf_op jit(solution)/shard_map/all_to_all | solution.py:450
  100.2 0.0 copy-done
  100.2 2.8 %shard_map.101 = (f32[16,1024]{1,0:T(8,128)}, f32[16,1024]{1,0:T(8,128)}) custom-call(s32[2]{0:T(128)} %parent_hbm.7, bf16[1024,1024]{1,0:T(8,128)(2,1)S(1)} %copy-done, f32[8,72,128]{2,1,0:T(8,128)S(1)} %all_to_all.22.got_ref, bf16[2,2,64,512]{3,2,1,0:T(8,128)(2,1)S(1)} %get-tuple-element.37.phi_ref, f32[16,1024]{1,0:T(8,128)S(1)} %get-tuple-element.46.local_ref, ...), custom_call_target="tpu_custom_call" | custom-call | tf_op jit(solution)/shard_map/pallas_call | solution.py:434
Async XLA Ops:
  1.5 14.6 %collective-permute-start.1 = (f32[24,1024]{1,0:T(8,128)S(1)}, f32[24,1024]{1,0:T(8,128)S(1)}, u32[]{:S(2)}, u32[]{:S(2)}) collective-permute-start(f32[24,1024]{1,0:T(8,128)S(1)} %get-tuple-element.26.packed_ref), channel_id=1, source_target_pairs={{4,0},{8,4},{12,8},{16,12},{20,16},{24,20},{28,24},{32,28},{36,32}... | collective-permute-start | bytes 294920 | tf_op jit(solution)/shard_map/ppermute | solution.py:443
  10.3 5.8 %collective-permute-start = (f32[24,1024]{1,0:T(8,128)S(1)}, f32[24,1024]{1,0:T(8,128)S(1)}, u32[]{:S(2)}, u32[]{:S(2)}) collective-permute-start(f32[24,1024]{1,0:T(8,128)S(1)} %get-tuple-element.26.packed_ref), channel_id=1, source_target_pairs={{0,4},{4,8},{8,12},{12,16},{16,20},{20,24},{24,28},{28,32},{32,36}... | collective-permute-start | bytes 294920 | tf_op jit(solution)/shard_map/ppermute | solution.py:442
  21.0 18.5 %all-to-all-start = ((f32[16,24,128]{2,1,0:T(8,128)}), f32[16,24,128]{2,1,0:T(8,128)S(1)}, u32[]{:S(2)}, u32[]{:S(2)}) async-start(f32[16,24,128]{2,1,0:T(8,128)} %get-tuple-element.34), calls=%async_computation | async-start | bytes 393216 | tf_op jit(solution)/shard_map/all_to_all | solution.py:448
  29.3 10.5 %collective-permute-start.3 = (f32[208,128]{1,0:T(8,128)S(1)}, f32[208,128]{1,0:T(8,128)S(1)}, u32[]{:S(2)}, u32[]{:S(2)}) collective-permute-start(f32[208,128]{1,0:T(8,128)S(1)} %get-tuple-element.35), channel_id=1, source_target_pairs={{4,0},{8,4},{12,8},{16,12},{20,16},{24,20},{28,24},{32,28},{36,32}... | collective-permute-start | bytes 319496 | tf_op jit(solution)/shard_map/ppermute | solution.py:443
  31.3 8.5 %collective-permute-start.2 = (f32[208,128]{1,0:T(8,128)S(1)}, f32[208,128]{1,0:T(8,128)S(1)}, u32[]{:S(2)}, u32[]{:S(2)}) collective-permute-start(f32[208,128]{1,0:T(8,128)S(1)} %get-tuple-element.35), channel_id=1, source_target_pairs={{0,4},{4,8},{8,12},{12,16},{16,20},{20,24},{24,28},{28,32},{32,36}... | collective-permute-start | bytes 319496 | tf_op jit(solution)/shard_map/ppermute | solution.py:442
  57.7 42.6 %copy-start = (bf16[1024,1024]{1,0:T(8,128)(2,1)S(1)}, bf16[1024,1024]{1,0:T(8,128)(2,1)}, u32[]{:S(2)}) copy-start(bf16[1024,1024]{1,0:T(8,128)(2,1)} %coupling_ref.1) | copy-start | bytes 6291460
where the time goes:
time: 104 us; the launch traced here: 103 us
  blocking collectives  50.8 us (49%)
  starting transfers between devices  24.5 us (24%)
  Pallas kernels  22.3 us (21%)
  waiting for transfers between devices  4.65 us (4%)
    all_to_all x2, blocking collectives, exchange(): return (lax.all_to_all(column, 'y', 0, 0, tiled=True), *ready)  33.3 us
    all_to_all x1, blocking collectives, exchange(): row = lax.all_to_all(send, ('z', 'c'), 0, 0, tiled=True)  17.5 us
    ppermute x2, starting transfers between devices, beside(): after = lax.ppermute(x, AXES, [(i + 1, i) for i in range(count - 1)])  10.8 us
    pallas_call x1, Pallas kernels, second(): call(second_kernel, [HBM] * 3 + [VMEM] * len(arrays), (shaped(16, SPAN),...  9.26 us
    all_to_all x1, starting transfers between devices, exchange(): row = lax.all_to_all(send, ('z', 'c'), 0, 0, tiled=True)  8.28 us
    ppermute x2, starting transfers between devices, beside(): before = lax.ppermute(x, AXES, [(i, i + 1) for i in range(count - 1)])  5.46 us
    pallas_call x1, Pallas kernels, first(): call(first_kernel, [HBM] * 2 + [VMEM] * 7, (shaped(4, LEAF, 64, dtype=BF1...  4.86 us
    all_to_all x1, waiting for transfers between devices, exchange(): row = lax.all_to_all(send, ('z', 'c'), 0, 0, tiled=True)  4.64 us
  transfers between devices with their start and end apart: 5, of which 1 were waited for; matrix products, arithmetic and copies ran while one was open for 0% of the time, Pallas kernels for 4%

commit v1 on v0

--- a/solution.py
+++ b/solution.py
@@ -81,7 +81,7 @@
 LIMIT = 24 * 1024 * 1024
 PAIRS = 4
 ROWS_OUT = 24
-ROWS_ACROSS = 16 * PAIRS + 8
+ROWS_ACROSS = 8 * PAIRS + 8
 TAIL = 80
 BESIDE = 128 + TAIL
 
@@ -181,22 +181,24 @@
 
 
 def across_kernel(got_ref, send_ref):
+    offset = (PAIRS * lax.axis_index("c")).astype(F32)
     lane = lax.broadcasted_iota(jnp.int32, (1, 128), 1)
     first = got_ref[0, 16:17, 4:5]
-    tiles = [jnp.zeros((16, 128), F32) for _ in range(2 * PAIRS)]
+    begin = first + offset
+    tiles = [jnp.zeros((16, 128), F32) for _ in range(PAIRS)]
     scalars = jnp.zeros((8, 128), F32)
     for d in range(got_ref.shape[0]):
-        slot = jnp.where(lane < 64, got_ref[d, 16:17, 4:5], got_ref[d, 16:17, 5:6]) - first
+        slot = jnp.where(lane < 64, got_ref[d, 16:17, 4:5], got_ref[d, 16:17, 5:6]) - begin
         piece = got_ref[d, :16, :]
-        for s in range(2 * PAIRS):
+        for s in range(PAIRS):
             tiles[s] = tiles[s] + jnp.where(slot == float(s), piece, 0.0)
         scalars = scalars + got_ref[d, 16:, :]
     scalars = jnp.where(lane == 4, first, scalars)
     tiles = paired(tiles)
     for y in range(send_ref.shape[0]):
-        for k in range(PAIRS):
+        for k in range(PAIRS // 2):
             send_ref[y, 16 * k : 16 * (k + 1), :] = tiles[k]
-        send_ref[y, 16 * PAIRS :, :] = scalars
+        send_ref[y, 8 * PAIRS :, :] = scalars
 
 
 def whole_sums(got_ref):
@@ -204,14 +206,15 @@
     half = (lane >= 64).astype(F32)
     tiles = [jnp.zeros((16, 128), F32) for _ in range(LEVELS)]
     scalars = jnp.zeros((8, 128), F32)
-    for y in range(got_ref.shape[0]):
-        first = got_ref[y, 16 * PAIRS : 16 * PAIRS + 1, 4:5] + half
-        for k in range(PAIRS):
-            piece = got_ref[y, 16 * k : 16 * (k + 1), :]
-            cluster = first + float(2 * k)
-            for q in range(LEVELS):
-                tiles[q] = tiles[q] + jnp.where(cluster == float(q), piece, 0.0)
-        scalars = scalars + got_ref[y, 16 * PAIRS :, :]
+    for y in range(got_ref.shape[1]):
+        first = got_ref[0, y, 8 * PAIRS : 8 * PAIRS + 1, 4:5] + half
+        for c in range(got_ref.shape[0]):
+            for k in range(PAIRS // 2):
+                piece = got_ref[c, y, 16 * k : 16 * (k + 1), :]
+                cluster = first + float(PAIRS * c + 2 * k)
+                for q in range(LEVELS):
+                    tiles[q] = tiles[q] + jnp.where(cluster == float(q), piece, 0.0)
+        scalars = scalars + got_ref[0, y, 8 * PAIRS :, :]
     norm = jnp.concatenate([scalars[:, 0:1], scalars[:, 2:3]], axis=0)
     inner = jnp.concatenate([scalars[:, 1:2], scalars[:, 3:4]], axis=0)
     return jnp.concatenate(paired(tiles), axis=1), norm, inner
@@ -310,15 +313,15 @@
     )(*off_chip(parent, mask), packed, skeleton, transfer, noise)
 
 
-def first_kernel(parent_hbm, mask_hbm, before_ref, after_ref, right_ref, part_ref, up_ref, packed_ref, tail_ref,
+def first_kernel(parent_hbm, mask_hbm, partner_ref, cross_ref, right_ref, part_ref, up_ref, packed_ref, tail_ref,
                  left_out, right_out, local_ref, beside_ref, send_ref, parent_ref, mask_ref, v_scr, acc_scr, k_scr, sems):
     flags = fetch(((parent_hbm, parent_ref), (mask_hbm, mask_ref)), sems)
-    for g, ref in enumerate((before_ref, after_ref)):
-        left, right = features(ref[:DIM, :])
+    for g, beyond in enumerate(ordered(partner_ref[...], cross_ref[...])):
+        left, right = features(beyond[:DIM, :])
         for i in range(LEAVES_HERE):
             left_out[2 * g + i] = left[:, leaf(i)].T.astype(BF16)
             right_out[2 * g + i] = right[:, leaf(i)].astype(BF16)
-            v_scr[4 * g + i] = halves(ref[DIM:, leaf(i)])
+            v_scr[4 * g + i] = halves(beyond[DIM:, leaf(i)])
     for i in range(LEAVES_HERE):
         acc_scr[i] = part_ref[:, leaf(i)]
     beside_ref[128:, :] = tail_ref[...]
@@ -333,7 +336,7 @@
     post(parent_ref, up_ref[...], packed_ref[DIM:, :], local, send_ref)
 
 
-def first(parent, mask, before, after, right, part, up, packed, tail, peers):
+def first(parent, mask, partner, cross, right, part, up, packed, tail, peers):
     return call(
         first_kernel, [HBM] * 2 + [VMEM] * 7,
         (
@@ -343,7 +346,7 @@
         FLAGS + [
             pltpu.VMEM((6, 32, LEAF), BF16), pltpu.VMEM((2, 16, LEAF), F32), pltpu.VMEM((SLOTS_KEPT, 2, LEAF, LEAF), BF16), pltpu.SemaphoreType.DMA((2,)),
         ],
-    )(*off_chip(parent, mask), before, after, right, part, up, packed, tail)
+    )(*off_chip(parent, mask), partner, cross, right, part, up, packed, tail)
 
 
 def across(got, rows):
@@ -351,14 +354,15 @@
 
 
 def second_kernel(parent_hbm, mask_hbm, coupling_hbm, got_ref, phi_ref, local_ref, packed_ref, diag_ref,
-                  before_ref, after_ref, halo_before_ref, halo_after_ref, left_ref, right_ref,
+                  partner_ref, cross_ref, partner_msg_ref, cross_msg_ref, left_ref, right_ref,
                   halo_left_ref, halo_right_ref,
                   residual_ref, along_ref, kept_ref, out_ref, send_ref,
                   parent_ref, mask_ref, coupling_scr, img_scr, v_scr, acc_scr, k_scr, bt_scr, sems):
     copies = fetch(((coupling_hbm, coupling_scr), (parent_hbm, parent_ref), (mask_hbm, mask_ref)), sems)
-    sides = ((halo_before_ref, before_ref), (halo_after_ref, after_ref))
-    for g, (msg_ref, _) in enumerate(sides):
-        sk_left, _ = features(msg_ref[192:200, :])
+    messages = ordered(partner_msg_ref[...], cross_msg_ref[...])
+    beyond = ordered(partner_ref[DIM:, :], cross_ref[DIM:, :])
+    for g, msg in enumerate(messages):
+        sk_left, _ = features(msg[192:200, :])
         for i in range(LEAVES_HERE):
             rows = sk_left[:, RANK * i : RANK * (i + 1)].T.astype(BF16)
             bt = matern(rows, halo_right_ref[2 * g + i]) * (1.0 / math.sqrt(LEAF))
@@ -376,10 +380,10 @@
     kept_ref[...] = jnp.where(lane == 0, norm, jnp.where(lane == 1, step, 0.0))
     for i in range(LEAVES_HERE):
         v_scr[2 + i] = halves(residual[:, leaf(i)])
-    for g, (msg_ref, ref) in enumerate(sides):
+    for g, msg in enumerate(messages):
         for i in range(LEAVES_HERE):
-            parent = jnp.max(msg_ref[200:208, RANK * i : RANK * (i + 1)]).astype(jnp.int32)
-            moved = msg_ref[128:192, RANK * i : RANK * (i + 1)].astype(BF16)
+            parent = jnp.max(msg[200:208, RANK * i : RANK * (i + 1)]).astype(jnp.int32)
+            moved = msg[128:192, RANK * i : RANK * (i + 1)].astype(BF16)
             pushed = jnp.zeros((16, RANK), F32)
             parts = lax.dot_general(
                 jnp.concatenate(split(img_scr[parent], 3), axis=0).astype(BF16), moved, (((1,), (1,)), ((), ())),
@@ -387,8 +391,8 @@
             )
             pushed = parts[:16] + parts[16:32] + parts[32:]
             far = pair_dot(pushed, bt_scr[2 * g + i, 0], bt_scr[2 * g + i, 1])
-            local = jnp.concatenate([msg_ref[16 * n : 16 * (n + 1), :] for n in range(4 * i, 4 * (i + 1))], axis=1)
-            v_scr[4 * g + i] = halves(ref[DIM:, leaf(i)] - step * (local + far))
+            local = jnp.concatenate([msg[16 * n : 16 * (n + 1), :] for n in range(4 * i, 4 * (i + 1))], axis=1)
+            v_scr[4 * g + i] = halves(beyond[g][:, leaf(i)] - step * (local + far))
     up = lifted(residual, phi_ref)
     acc_scr[...] = jnp.zeros(acc_scr.shape, F32)
     near_field(4, own_block, mask_ref, lambda j, rows: left_ref[j - 2, rows, :], lambda i: right_ref[i], v_scr, acc_scr, k_scr)
@@ -439,30 +443,36 @@
 
 def beside(x):
     count = lax.axis_size(AXES)
-    before = lax.ppermute(x, AXES, [(i, i + 1) for i in range(count - 1)])
-    after = lax.ppermute(x, AXES, [(i + 1, i) for i in range(count - 1)])
-    return before, after
+    swaps = [(i, i ^ 1) for i in range(count)]
+    crossings = [(i, i + 1 if i % 2 else i - 1) for i in range(1, count - 1)]
+    cross = lax.ppermute(x, AXES, crossings)
+    return lax.ppermute(x, AXES, swaps), cross
+
+
+def ordered(partner, cross):
+    core = lax.axis_index("c")
+    return jnp.where(core == 0, cross, partner), jnp.where(core == 0, partner, cross)
 
 
 def exchange(send, *ready):
     row = lax.all_to_all(send, ("z", "c"), 0, 0, tiled=True)
     column, *ready = lax.optimization_barrier((across(row, lax.axis_size("y")), *ready))
-    return lax.all_to_all(column, "y", 0, 0, tiled=True), *ready
+    return lax.all_gather(lax.all_to_all(column, "y", 0, 0, tiled=True), "c"), *ready
 
 
 def per_device(coords, skeleton, transfer, coupling, parent, near_mask, noise, rhs):
     peers = lax.axis_size(("z", "c"))
     packed, skeleton, transfer, noise = pack(coords, skeleton, transfer, noise.reshape(1, SPAN), rhs)
-    before, after = beside(packed)
+    partner, cross = beside(packed)
     left, right, phi, part, up, diag, tail = prepare(parent, near_mask, packed, skeleton, transfer, noise)
     halo_left, halo_right, local, message, send = first(
-        parent, near_mask, before, after, right, part, up, packed, tail, peers
-    )
-    halo_before, halo_after = beside(message)
-    got, halo_before, halo_after = exchange(send, halo_before, halo_after)
+        parent, near_mask, partner, cross, right, part, up, packed, tail, peers
+    )
+    partner_msg, cross_msg = beside(message)
+    got, partner_msg, cross_msg = exchange(send, partner_msg, cross_msg)
     residual, along, kept, local, send = second(
-        parent, near_mask, coupling, got, phi, local, packed, diag, before, after,
-        halo_before, halo_after, left, right, halo_left, halo_right, peers=peers,
+        parent, near_mask, coupling, got, phi, local, packed, diag, partner, cross,
+        partner_msg, cross_msg, left, right, halo_left, halo_right, peers=peers,
     )
     (got,) = exchange(send)
     return last(parent, coupling, got, phi, local, packed, residual, along, kept)

time: 104 us -> 98.9 us (0.951)
  blocking collectives: 50.8 us -> 47.3 us
  starting transfers between devices: 24.5 us -> 22.7 us
    all_gather x0 -> x2, blocking collectives: none -> 4.33 us  [exchange(): lax.all_gather(lax.all_to_all(column, 'y', 0, 0, tiled=True), 'c')]
    all_to_all x1, blocking collectives: 17.5 us -> 13.4 us  [exchange(): row = lax.all_to_all(send, ('z', 'c'), 0, 0, tiled=True)]
    all_to_all x2, blocking collectives: 33.3 us -> 29.6 us  [exchange(): lax.all_to_all(column, 'y', 0, 0, tiled=True)]
    ppermute x4, starting transfers between devices: 16.2 us -> 14.9 us  [the longest x2 8.91 us: beside(): cross = lax.ppermute(x, AXES, crossings)]
where the time goes in v1:
time: 98.9 us; the launch traced here: 98.4 us
  blocking collectives  47.3 us (48%)
  starting transfers between devices  22.7 us (23%)
  Pallas kernels  22.3 us (23%)
  waiting for transfers between devices  5.22 us (5%)
    all_to_all x2, blocking collectives, exchange(): lax.all_to_all(column, 'y', 0, 0, tiled=True)  29.6 us
    all_to_all x1, blocking collectives, exchange(): row = lax.all_to_all(send, ('z', 'c'), 0, 0, tiled=True)  13.4 us
    pallas_call x1, Pallas kernels, second(): call(second_kernel, [HBM] * 3 + [VMEM] * len(arrays), (shaped(16, SPAN),...  9.28 us
    ppermute x2, starting transfers between devices, beside(): cross = lax.ppermute(x, AXES, crossings)  8.91 us
    all_to_all x1, starting transfers between devices, exchange(): row = lax.all_to_all(send, ('z', 'c'), 0, 0, tiled=True)  7.81 us
    ppermute x2, starting transfers between devices, beside(): return (lax.ppermute(x, AXES, swaps), cross)  5.96 us
    all_to_all x1, waiting for transfers between devices, exchange(): row = lax.all_to_all(send, ('z', 'c'), 0, 0, tiled=True)  5.21 us
    pallas_call x1, Pallas kernels, first(): call(first_kernel, [HBM] * 2 + [VMEM] * 7, (shaped(4, LEAF, 64, dtype=BF1...  4.91 us
  transfers between devices with their start and end apart: 5, of which 1 were waited for; matrix products, arithmetic and copies ran while one was open for 0% of the time, Pallas kernels for 4%

profile of v1, /device:TPU:1, one launch (start us, length us, event | category | flops | bytes accessed | tf_op | source)
XLA Modules:
  0.0 98.4 jit_solution(2006612523651859332)
XLA Ops:
  0.6 0.9 shard_map.95
  1.5 5.4 %collective-permute-start.1 = (f32[24,1024]{1,0:T(8,128)S(1)}, f32[24,1024]{1,0:T(8,128)S(1)}, u32[]{:S(2)}, u32[]{:S(2)}) collective-permute-start(f32[24,1024]{1,0:T(8,128)S(1)} %get-tuple-element.26.packed_ref), channel_id=1, source_target_pairs={{4,8},{8,4},{12,16},{16,12},{20,24},{24,20},{28,32},{32,28},{36,40... | collective-permute-start | bytes 294920 | tf_op jit(solution)/shard_map/ppermute | solution.py:448
  6.9 4.0 %collective-permute-start = (f32[24,1024]{1,0:T(8,128)S(1)}, f32[24,1024]{1,0:T(8,128)S(1)}, u32[]{:S(2)}, u32[]{:S(2)}) collective-permute-start(f32[24,1024]{1,0:T(8,128)S(1)} %get-tuple-element.26.packed_ref), channel_id=1, source_target_pairs={{0,4},{4,0},{8,12},{12,8},{16,20},{20,16},{24,28},{28,24},{32,36},... | collective-permute-start | bytes 294920 | tf_op jit(solution)/shard_map/ppermute | solution.py:449
  11.0 3.9 %shard_map.96 = (bf16[2,512,64]{2,1,0:T(8,128)(2,1)S(1)}, bf16[2,64,512]{2,1,0:T(8,128)(2,1)S(1)}, bf16[2,2,64,512]{3,2,1,0:T(8,128)(2,1)S(1)}, f32[16,1024]{1,0...) custom-call(s32[2]{0:T(128)} %parent_hbm.7, s32[2,5]{1,0:T(2,128)} %mask_hbm.5, ...), custom_call_target="tpu_custom_call" | custom-call | tf_op jit(solution)/shard_map/pallas_call | solution.py:304
  14.9 0.0 collective-permute-done.1.cross_ref
  14.9 0.0 collective-permute-done.partner_ref
  14.9 4.9 %shard_map.97 = (bf16[4,512,64]{2,1,0:T(8,128)(2,1)S(1)}, bf16[4,64,512]{2,1,0:T(8,128)(2,1)S(1)}, f32[16,1024]{1,0:T(8,128)S(1)}, f32[208,128]{1,0:T(8,128)S(1)}, f32[16,24,128]{2,1,0:T(8,128)}) custom-call(s32[2]{0:T(128)} %parent_hbm.7, s32[2,5]{1,0:T(2,128)} %mask_hbm.5, f32[24,1024]{1,0:T(8,128)S(1)} %collective-permute-done.partner_ref, ...), custom_call_target="tpu_custom_call" | custom-call | tf_op jit(solution)/shard_map/pallas_call | solution.py:340
  19.8 7.8 %all-to-all-start = ((f32[16,24,128]{2,1,0:T(8,128)}), f32[16,24,128]{2,1,0:T(8,128)S(1)}, u32[]{:S(2)}, u32[]{:S(2)}) async-start(f32[16,24,128]{2,1,0:T(8,128)} %get-tuple-element.34), calls=%async_computation | async-start | bytes 393216 | tf_op jit(solution)/shard_map/all_to_all | solution.py:458
  27.6 3.5 %collective-permute-start.3 = (f32[208,128]{1,0:T(8,128)S(1)}, f32[208,128]{1,0:T(8,128)S(1)}, u32[]{:S(2)}, u32[]{:S(2)}) collective-permute-start(f32[208,128]{1,0:T(8,128)S(1)} %get-tuple-element.35), channel_id=1, source_target_pairs={{4,8},{8,4},{12,16},{16,12},{20,24},{24,20},{28,32},{32,28},{36,40... | collective-permute-start | bytes 319496 | tf_op jit(solution)/shard_map/ppermute | solution.py:448
  31.1 1.9 %collective-permute-start.2 = (f32[208,128]{1,0:T(8,128)S(1)}, f32[208,128]{1,0:T(8,128)S(1)}, u32[]{:S(2)}, u32[]{:S(2)}) collective-permute-start(f32[208,128]{1,0:T(8,128)S(1)} %get-tuple-element.35), channel_id=1, source_target_pairs={{0,4},{4,0},{8,12},{12,8},{16,20},{20,16},{24,28},{28,24},{32,36},... | collective-permute-start | bytes 319496 | tf_op jit(solution)/shard_map/ppermute | solution.py:449
  33.1 5.2 %all-to-all-done.got_ref = f32[16,24,128]{2,1,0:T(8,128)S(1)} async-done(((f32[16,24,128]{2,1,0:T(8,128)}), f32[16,24,128]{2,1,0:T(8,128)S(1)}, u32[]{:S(2)}, u32[]{:S(2)}) %all-to-all-start) | async-done | bytes 196640 | tf_op jit(solution)/shard_map/all_to_all | solution.py:458
  38.3 0.2 shard_map.98
  38.5 0.0 collective-permute-done.3.cross_msg_ref
  38.5 0.0 collective-permute-done.2.partner_msg_ref
  38.5 16.9 %all_to_all.20 = f32[8,40,128]{2,1,0:T(8,128)S(1)} all-to-all(f32[8,40,128]{2,1,0:T(8,128)S(1)} %shard_map.98), channel_id=1, replica_groups=mesh['y'=8,'z'=8,'c'=2,'rep'=4] {'y'}, dimensions={0} | all-to-all | bytes 327680 | tf_op jit(solution)/shard_map/all_to_all | solution.py:460
  55.5 2.3 %all-gather = f32[16,40,128]{2,1,0:T(8,128)S(1)} all-gather(f32[8,40,128]{2,1,0:T(8,128)S(1)} %all_to_all.20), channel_id=2, replica_groups=mesh['y'=8,'z'=8,'c'=2,'rep'=4] {'c'}, dimensions={0}, use_global_device_ids=true | all-gather | bytes 491520 | tf_op jit(solution)/shard_map/all_gather | solution.py:460
  57.7 0.0 copy-start
  57.7 9.3 %shard_map.99 = (f32[16,1024]{1,0:T(8,128)S(1)}, f32[16,1024]{1,0:T(8,128)S(1)}, f32[16,128]{1,0:T(8,128)S(1)}, f32[16,1024]{1,0:T(8,128)S(1)}, f32[16,24,128]{2,1,0:T(8,128)S(1)}) custom-call(s32[2]{0:T(128)} %parent_hbm.7, s32[2,5]{1,0:T(2,128)} %mask_hbm.5, bf16[1024,1024]{1,0:T(8,128)(2,1)} %coupling_ref.1, f32[2,8,40,128]{3,2,1,0:T(8,128)S(1)} %bitcast.3, ...), custom_call_target="tpu_custom_call" | custom-call | tf_op jit(solution)/shard_map/pallas_call | solution.py:408
  67.0 13.4 %all_to_all.21.got_ref = f32[16,24,128]{2,1,0:T(8,128)S(1)} all-to-all(f32[16,24,128]{2,1,0:T(8,128)S(1)} %get-tuple-element.45), channel_id=1, replica_groups=mesh['y'=8,'z'=8,'c'=2,'rep'=4] {'z','c'}, dimensions={0} | all-to-all | bytes 393216 | tf_op jit(solution)/shard_map/all_to_all | solution.py:458
  80.4 0.2 shard_map.100
  80.6 12.7 %all_to_all.22 = f32[8,40,128]{2,1,0:T(8,128)S(1)} all-to-all(f32[8,40,128]{2,1,0:T(8,128)S(1)} %shard_map.100), channel_id=1, replica_groups=mesh['y'=8,'z'=8,'c'=2,'rep'=4] {'y'}, dimensions={0} | all-to-all | bytes 327680 | tf_op jit(solution)/shard_map/all_to_all | solution.py:460
  93.3 2.1 %all-gather.1 = f32[16,40,128]{2,1,0:T(8,128)S(1)} all-gather(f32[8,40,128]{2,1,0:T(8,128)S(1)} %all_to_all.22), channel_id=3, replica_groups=mesh['y'=8,'z'=8,'c'=2,'rep'=4] {'c'}, dimensions={0}, use_global_device_ids=true | all-gather | bytes 491520 | tf_op jit(solution)/shard_map/all_gather | solution.py:460
  95.4 0.0 copy-done
  95.4 2.8 %shard_map.101 = (f32[16,1024]{1,0:T(8,128)}, f32[16,1024]{1,0:T(8,128)}) custom-call(s32[2]{0:T(128)} %parent_hbm.7, bf16[1024,1024]{1,0:T(8,128)(2,1)S(1)} %copy-done, f32[2,8,40,128]{3,2,1,0:T(8,128)S(1)} %bitcast.4, bf16[2,2,64,512]{3,2,1,0:T(8,128)(2,1)S(1)} %get-tuple-element.37.phi_ref, f32[16,1024]{1,0:T(8,128)S(1)} %get-tuple-element.46.local_ref, ...), custom_call_target="tpu_custom_call" | custom-call | tf_op jit(solution)/shard_map/pallas_call | solution.py:438
Async XLA Ops:
  1.5 13.3 %collective-permute-start.1 = (f32[24,1024]{1,0:T(8,128)S(1)}, f32[24,1024]{1,0:T(8,128)S(1)}, u32[]{:S(2)}, u32[]{:S(2)}) collective-permute-start(f32[24,1024]{1,0:T(8,128)S(1)} %get-tuple-element.26.packed_ref), channel_id=1, source_target_pairs={{4,8},{8,4},{12,16},{16,12},{20,24},{24,20},{28,32},{32,28},{36,40... | collective-permute-start | bytes 294920 | tf_op jit(solution)/shard_map/ppermute | solution.py:448
  6.9 7.9 %collective-permute-start = (f32[24,1024]{1,0:T(8,128)S(1)}, f32[24,1024]{1,0:T(8,128)S(1)}, u32[]{:S(2)}, u32[]{:S(2)}) collective-permute-start(f32[24,1024]{1,0:T(8,128)S(1)} %get-tuple-element.26.packed_ref), channel_id=1, source_target_pairs={{0,4},{4,0},{8,12},{12,8},{16,20},{20,16},{24,28},{28,24},{32,36},... | collective-permute-start | bytes 294920 | tf_op jit(solution)/shard_map/ppermute | solution.py:449
  19.8 18.5 %all-to-all-start = ((f32[16,24,128]{2,1,0:T(8,128)}), f32[16,24,128]{2,1,0:T(8,128)S(1)}, u32[]{:S(2)}, u32[]{:S(2)}) async-start(f32[16,24,128]{2,1,0:T(8,128)} %get-tuple-element.34), calls=%async_computation | async-start | bytes 393216 | tf_op jit(solution)/shard_map/all_to_all | solution.py:458
  27.6 10.9 %collective-permute-start.3 = (f32[208,128]{1,0:T(8,128)S(1)}, f32[208,128]{1,0:T(8,128)S(1)}, u32[]{:S(2)}, u32[]{:S(2)}) collective-permute-start(f32[208,128]{1,0:T(8,128)S(1)} %get-tuple-element.35), channel_id=1, source_target_pairs={{4,8},{8,4},{12,16},{16,12},{20,24},{24,20},{28,32},{32,28},{36,40... | collective-permute-start | bytes 319496 | tf_op jit(solution)/shard_map/ppermute | solution.py:448
  31.1 7.4 %collective-permute-start.2 = (f32[208,128]{1,0:T(8,128)S(1)}, f32[208,128]{1,0:T(8,128)S(1)}, u32[]{:S(2)}, u32[]{:S(2)}) collective-permute-start(f32[208,128]{1,0:T(8,128)S(1)} %get-tuple-element.35), channel_id=1, source_target_pairs={{0,4},{4,0},{8,12},{12,8},{16,20},{20,16},{24,28},{28,24},{32,36},... | collective-permute-start | bytes 319496 | tf_op jit(solution)/shard_map/ppermute | solution.py:449
  57.7 37.7 %copy-start = (bf16[1024,1024]{1,0:T(8,128)(2,1)S(1)}, bf16[1024,1024]{1,0:T(8,128)(2,1)}, u32[]{:S(2)}) copy-start(bf16[1024,1024]{1,0:T(8,128)(2,1)} %coupling_ref.1) | copy-start | bytes 6291460
